TPU v7x, 32 devices: a whole 2x2x4 slice. The times are simulated.
32 devices in a mesh: expert: 8 (over y, x, core), row: 4 (over z).
Axes of the slice: x: 2, y: 2, z: 4, core: 2. Of those that a mesh axis runs over, the one named last changes fastest.
Arguments:
- weights: bfloat16 [8, 7168, 2048], P('expert', 'row'), may hold values from -6 to 6
- left_bits: int32 [8, 7168], P('expert', 'row'), may hold values from 0 to 1
- right_bits: int32 [8, 2048], P('expert'), may hold values from 0 to 1
- groups: int32 [8, 2048], P('expert'), may hold values from 0 to 15, never falling along the last dimension, each value on 1 to 256 neighbouring positions
Outputs:
- scaled: bfloat16 [8, 7168, 2048], P('expert', 'row')
- block_error: float32 [8, 7168, 256], P('expert', 'row')
- scales: float32 [8, 16], P('expert')
- expert_error: float32 [8], P('expert')
- total_error: float32 [], replicated
Inputs may be any that keep to these rules, and one draw needn't show every extreme that they name: Along each expert's 2048 columns the group number never falls; each of the 16 groups holds 1 to 256 columns.
All inputs are finite; a program needn't handle non-finite values.
Results may differ from a plain program's by a relative error of at most 0.0091.
Values may be sent and summed in bfloat16 or wider, within the bound.
A program may use at most 192 MiB of HBM per device.

v0:
```python
import math

import jax
import jax.numpy as jnp
from jax import lax
from jax.sharding import PartitionSpec as P

D = 7168
FF = 2048
HB = 128
OUTER = 16
GROUPS = 16
BLOCKS = 56


def sylvester(order):
    row_index = jnp.arange(order, dtype=jnp.int32)[:, None]
    col_index = jnp.arange(order, dtype=jnp.int32)[None, :]
    common = jnp.bitwise_and(row_index, col_index)
    parity = jnp.zeros((order, order), jnp.int32)
    for bit_pos in range(order.bit_length() - 1):
        parity = parity + jnp.bitwise_and(jnp.right_shift(common, bit_pos), 1)
    return (1 - 2 * jnp.bitwise_and(parity, 1)).astype(jnp.float32)


def cosine_block(order):
    first = jnp.arange(order, dtype=jnp.float32)[:, None]
    second = jnp.arange(order, dtype=jnp.float32)[None, :]
    table = math.sqrt(2.0 / order) * jnp.cos(math.pi * (2.0 * second + 1.0) * first / (2.0 * order))
    return jnp.where(first == 0.0, table * math.sqrt(0.5), table)


def coset_error(values):
    nearest = jnp.floor(values + 0.5)
    offset = values - nearest
    squares = jnp.sum(offset * offset, axis=-1)
    largest = jnp.max(jnp.abs(offset), axis=-1)
    parity = jnp.mod(jnp.sum(nearest, axis=-1), 2.0)
    return jnp.where(parity > 0.5, squares + 1.0 - 2.0 * largest, squares)


def lattice_error(values):
    octets = values.reshape(values.shape[:-1] + (values.shape[-1] // 8, 8))
    return jnp.minimum(coset_error(octets), coset_error(octets - 0.5))


def row_transform(mixed_rows, row_hadamard):
    turned = jnp.einsum("eibf,bk->eikf", mixed_rows, row_hadamard, precision=lax.Precision.HIGHEST)
    return turned / math.sqrt(HB)


def weight_of_rows(first_row, count):
    positions = (first_row + jnp.arange(count, dtype=jnp.int32)).astype(jnp.float32)
    return (1.0 + 4.0 * (positions + 0.5) / D) / 3.0


def group_scale(rotated, group_cols):
    column_peak = jnp.max(jnp.abs(rotated), axis=1)
    group_ids = jnp.arange(GROUPS, dtype=jnp.int32)
    in_group = group_cols[:, None, :] == group_ids[None, :, None]
    partial_peak = jnp.max(jnp.where(in_group, column_peak[:, None, :], 0.0), axis=2)
    group_peak = jnp.maximum(lax.pmax(partial_peak, "row"), 1.0)
    column_scale = jnp.sum(jnp.where(in_group, (2.0 / group_peak)[:, :, None], 0.0), axis=1)
    return (group_peak, column_scale)


def body(weights, left_bits, right_bits, groups):
    experts, local_rows, width = weights.shape
    blocks_here = local_rows // HB
    column_hadamard = sylvester(width // OUTER).astype(jnp.bfloat16)
    outer_hadamard = sylvester(OUTER)
    row_hadamard = sylvester(HB)
    block_matrix = cosine_block(BLOCKS).astype(jnp.bfloat16)
    left_sign = (2 * left_bits - 1).astype(jnp.float32)
    right_sign = (2 * right_bits - 1).astype(jnp.float32)
    signed = (weights.astype(jnp.float32) * left_sign[:, :, None] * right_sign[:, None, :]).astype(
        jnp.bfloat16
    )
    shaped = signed.reshape(experts, local_rows, OUTER, width // OUTER)
    inner = jnp.einsum("erpq,qs->erps", shaped, column_hadamard, preferred_element_type=jnp.float32)
    outer = jnp.einsum("erps,pt->erts", inner, outer_hadamard, precision=lax.Precision.HIGHEST)
    columns = (outer.reshape(experts, local_rows, width) / math.sqrt(FF)).astype(jnp.bfloat16)
    blocked = columns.reshape(experts, blocks_here, HB, width)
    own_start = lax.axis_index("row") * blocks_here
    own_matrix = lax.dynamic_slice_in_dim(block_matrix, own_start, blocks_here, 0)
    mixed_rows = jnp.einsum(
        "ij,ejbf->eibf",
        own_matrix,
        lax.all_gather(blocked, "row", axis=1, tiled=True),
        preferred_element_type=jnp.float32,
    )
    rotated = row_transform(mixed_rows, row_hadamard)
    rotated = rotated.reshape(experts, local_rows, width)
    group_peak, column_scale = group_scale(rotated, groups)
    values = rotated * column_scale[:, None, :]
    block_errors = lattice_error(values)
    row_weight = weight_of_rows(lax.axis_index("row") * local_rows, local_rows)
    partial_error = jnp.sum(block_errors * row_weight[None, :, None], axis=(1, 2)) / (D * FF // 8)
    scaled = values.astype(jnp.bfloat16)
    expert_count = experts * lax.axis_size("expert")
    expert_error = lax.psum(partial_error, "row")
    total_error = lax.psum(jnp.sum(expert_error), "expert") / expert_count
    return (scaled, block_errors, group_peak / 2.0, expert_error, total_error)


def solution(mesh):
    placed = (P("expert", "row", None), P("expert", "row"), P("expert", None), P("expert", None))
    return jax.shard_map(
        body,
        mesh=mesh,
        in_specs=placed,
        out_specs=(
            P("expert", "row", None),
            P("expert", "row", None),
            P("expert", None),
            P("expert"),
            P(),
        ),
        check_vma=False,
    )
```

profile of v0, /device:TPU:0, one launch (start us, length us, event | category | flops | bytes accessed | tf_op | source)
XLA Modules:
  0.0 734.2 jit_solution(6547402217888224501)
XLA Ops:
  7.2 0.0 all-gather.2.cloned.1.call-start
  7.2 0.7 add_convert_fusion
  7.9 0.7 convert_reduce_fusion
  8.6 5.1 fusion.8
  13.7 5.8 copy.28
  19.5 4.3 fusion.25
  23.9 15.7 %fusion.14 = bf16[1,1792,16,128]{3,2,1,0:T(8,128)(2,1)} fusion(f32[1792,16,128]{2,1,0:T(8,128)S(1)} %fusion.25), kind=kOutput, calls=%fused_computation.22 | convolution fusion | flops 711987200 | bytes 22020096 | tf_op jit(solution)/shard_map/erps,pt->erts/dot_general | solution.py:81
  39.6 11.8 %convert_element_type.76 = bf16[1,14,128,2048]{3,2,1,0:T(8,128)(2,1)} reshape(bf16[1,1792,16,128]{3,2,1,0:T(8,128)(2,1)} %fusion.14) | data formatting | bytes 14680064 | tf_op jit(solution)/shard_map/convert_element_type | solution.py:82
  51.4 0.0 all-gather.2.cloned.1.call-update
  51.4 0.1 dynamic-slice
  51.5 495.9 %all-gather.2.cloned.1.call-done = bf16[1,56,128,2048]{3,2,0,1:T(8,128)(2,1)} async-done(((bf16[1,14,128,2048]{3,2,0,1:T(8,128)(2,1)}), bf16[1,56,128,2048]{3,2,0,1:T(8,128)(2,1)}) %all-gather.2.cloned.1.call-update) | async-done | bytes 29360144 | tf_op jit(solution)/shard_map/all_gather | solution.py:89
  547.4 31.9 %fusion.9 = f32[14,128,2048]{2,0,1:T(8,128)} fusion(bf16[1,56,128,2048]{3,2,0,1:T(8,128)(2,1)} %all-gather.2.cloned.1.call-done, s32[]{:T(128)S(6)} %select_n.94, f32[56]{0:T(128)S(1)} %add_multiply_fusion.2, pred[14]{0:T(512)(128)(4,1)S(1)} %dynamic-slice), kind=kOutput, calls=%fused_computation.21 | convolution fusion | flops 411048064 | bytes 44040432 | tf_op jit(solution)/shard_map/ij,ejbf->eibf/dot_general | solution.py:86
  579.3 0.0 copy-start
  579.3 29.6 %abs_reduce_fusion.2 = (f32[2048]{0:T(1024)S(1)}, f32[128,14,2048]{2,0,1:T(8,128)}) fusion(f32[14,128,2048]{2,0,1:T(8,128)} %fusion.9), kind=kOutput, calls=%fused_computation.15 | convolution fusion | flops 5648562176 | bytes 29368320 | tf_op jit(solution)/shard_map/eibf,bk->eikf/dot_general | solution.py:48
  608.9 0.0 copy-done
  608.9 0.1 select_reduce_fusion.1
  609.0 8.9 %pmax.7 = f32[1,16]{1,0:T(1,128)S(1)} all-reduce(f32[1,16]{1,0:T(1,128)S(1)} %bitcast.114), channel_id=1, replica_groups=mesh['expert'=8,'row'=4] {'row'}, use_global_device_ids=true, to_apply=%region_2.3 | all-reduce | flops 16 | bytes 128 | tf_op jit(solution)/shard_map/pmax | solution.py:62
  617.9 0.5 maximum_multiply_fusion
  618.4 0.1 select_reduce_fusion
  618.5 0.1 mul.276
  618.6 10.4 %fusion.3 = bf16[1,1792,2048]{2,1,0:T(8,128)(2,1)} fusion(f32[128,14,2048]{2,0,1:T(8,128)} %get-tuple-element.26, f32[2048]{0:T(1024)S(1)} %select_reduce_fusion), kind=kLoop, calls=%fused_computation.4 | loop fusion | flops 7340032 | bytes 22028288 | tf_op jit(solution)/shard_map/convert_element_type | solution.py:99
  629.0 17.6 %copy.24 = f32[1,14,128,2048]{2,1,3,0:T(8,128)} copy(f32[1,14,128,2048]{3,2,1,0:T(8,128)} %bitcast.108) | data formatting | bytes 29360128 | tf_op jit(solution)/shard_map/div | solution.py:49
  646.6 16.9 %reshape.599 = f32[1,1792,256,8]{1,3,2,0:T(8,128)} reshape(f32[1,14,128,2048]{2,1,3,0:T(8,128)} %copy.24) | data formatting | bytes 29360128 | tf_op jit(solution)/shard_map/reshape | solution.py:93
  663.5 32.5 %fusion.7 = (f32[1792,256]{0,1:T(8,128)S(1)}, f32[1792,256]{0,1:T(8,128)S(1)}, f32[1792,256]{0,1:T(8,128)S(1)}, f32[1792,256]{0,1:T(8,128)S(1)}, f32[1792,256]{0,1:T(8,128)S(1)}, /*index=5*/f32[1792,256]{0,1:T(8,128)S(1)}) fusion(f32[1,1792,256,8]{1,3,2,0:T(8,128)} %reshape.599, f32[256,8]{1,0:T(8,128)S(1)} %mul.276), kind=kLoop, calls=%fused_computation.14 | loop fusion | flops 59637760 | bytes 25698304 | tf_op jit(solution)/shard_map/reduce_sum | solution.py:38
  696.0 3.2 multiply_reduce_fusion.2
  699.3 1.7 copy.25
  701.6 11.3 %psum.14 = f32[1]{0:T(128)} all-reduce(f32[1]{0:T(128)} %bitcast.25), channel_id=1, replica_groups=mesh['expert'=8,'row'=4] {'row'}, use_global_device_ids=true, to_apply=%region_11.12 | all-reduce | flops 1 | bytes 8 | tf_op jit(solution)/shard_map/psum | solution.py:101
  712.9 12.4 %psum.15 = f32[]{:T(128)} all-reduce(f32[]{:T(128)} %bitcast.26), channel_id=1, replica_groups=mesh['expert'=8,'row'=4] {'expert'}, use_global_device_ids=true, to_apply=%region_12.13 | all-reduce | flops 1 | bytes 8 | tf_op jit(solution)/shard_map/psum | solution.py:102
  (3 shorter events, 0.0 us)
Async XLA Ops:
  7.2 540.2 %all-gather.2.cloned.1.call-start = ((), (), s32[]{:S(2)}) async-start(), calls=%async_computation | async-start | bytes 36700160 | tf_op jit(solution)/shard_map/all_gather | solution.py:89
  579.3 29.6 %copy-start = (s32[1,2048]{1,0:T(1,128)S(1)}, s32[1,2048]{1,0:T(1,128)}, u32[]{:S(2)}) copy-start(s32[1,2048]{1,0:T(1,128)} %param.7) | copy-start | bytes 24580
Sparse Core Ops, SparseCore 0:
  51.5 495.8 all-gather.1
where the time goes:
time: 743 us; the launch traced here: 734 us
  waiting for transfers between devices  496 us (67%)
  matrix products  81.6 us (11%)
  local copies, waits for them, and re-layouts  53.9 us (7%)
  other arithmetic  53.5 us (7%)
  blocking collectives  32.6 us (4%)
  between operations  16.7 us (2%)
    all_gather x1, waiting for transfers between devices, body(): lax.all_gather(blocked, 'row', axis=1, tiled=True)  496 us
    reduce_sum x1, other arithmetic, coset_error(): parity = jnp.mod(jnp.sum(nearest, axis=-1), 2.0)  32.5 us
    dot_general x1, matrix products, body(): jnp.einsum('ij,ejbf->eibf', own_matrix, lax.all_gather(blocked, 'row', ax...  31.9 us
    dot_general x1, matrix products, row_transform(): jnp.einsum('eibf,bk->eikf', mixed_rows, row_hadamard, precision=lax.Preci...  29.6 us
    div x1, local copies, waits for them, and re-layouts, row_transform(): return turned / math.sqrt(HB)  17.6 us
    reshape x1, local copies, waits for them, and re-layouts, body(): rotated = rotated.reshape(experts, local_rows, width)  16.9 us
    dot_general x1, matrix products, body(): jnp.einsum('erps,pt->erts', inner, outer_hadamard, precision=lax.Precisio...  15.7 us
  transfers between devices with their start and end apart: 1, of which 1 were waited for; matrix products, arithmetic and copies ran while one was open for 0% of the time, Pallas kernels for 0%

commit v1 on v0

v1 whole, which is shorter than its diff:
```python
import functools
import math

import jax
import jax.numpy as jnp
from jax import lax
from jax.experimental import pallas as pl
from jax.experimental.pallas import tpu as pltpu
from jax.sharding import PartitionSpec as P

HB = 128
SUB = 16
FOLD = HB // SUB
OCT = 8
LANES = 128
GROUPS = 16
BLOCKS = 56
MESH = pl.DeviceIdType.MESH


def signs(common, bits):
    parity = common & 1
    for bit_pos in range(1, bits):
        parity = parity + ((common >> bit_pos) & 1)
    return (1 - 2 * (parity & 1)).astype(jnp.float32)


def cosine_block(order):
    first = jnp.arange(order, dtype=jnp.float32)[:, None]
    second = jnp.arange(order, dtype=jnp.float32)[None, :]
    table = math.sqrt(2.0 / order) * jnp.cos(math.pi * (2.0 * second + 1.0) * first / (2.0 * order))
    return jnp.where(first == 0.0, table * math.sqrt(0.5), table)


def column_matrix(right_bits, peers, half, scale):
    slabs = OCT // peers
    shape = (2, peers, half, slabs, LANES)
    row = lax.broadcasted_iota(jnp.int32, shape, 2)
    slab = lax.broadcasted_iota(jnp.int32, shape, 1) * slabs + lax.broadcasted_iota(jnp.int32, shape, 3)
    col = lax.broadcasted_iota(jnp.int32, shape, 4) * OCT + slab
    sign = (2 * right_bits - 1).astype(jnp.float32).reshape(2, 1, half, 1, 1)
    full = signs(row & col, half.bit_length() - 1) * sign * scale
    return full.astype(jnp.bfloat16).reshape(2, peers, half, slabs * LANES)


def row_matrix():
    cosine = cosine_block(BLOCKS).astype(jnp.bfloat16).astype(jnp.float32)
    index = jnp.arange(SUB, dtype=jnp.int32)
    small = signs(index[:, None] & index[None, :], SUB.bit_length() - 1)
    size = BLOCKS * SUB
    full = cosine[:, None, :, None] * small[None, :, None, :]
    return full.reshape(size, size).astype(jnp.bfloat16)


def order_matrix(half):
    source = lax.broadcasted_iota(jnp.int32, (half, half), 0)
    target = lax.broadcasted_iota(jnp.int32, (half, half), 1)
    wanted = (source % LANES) * OCT + source // LANES
    return (wanted == target).astype(jnp.bfloat16)


def fold_rows(parts):
    step = 1
    while step < len(parts):
        mixed = list(parts)
        for k in range(len(parts)):
            if not k & step:
                mixed[k] = parts[k] + parts[k + step]
                mixed[k + step] = parts[k] - parts[k + step]
        parts, step = mixed, 2 * step
    return parts


def kernel(
    peers, x_ref, left_ref, group_ref, h_ref, m_ref, p_ref,
    scaled_ref, error_ref, scale_ref, sum_ref,
    out1, in1, out2, in2, peaks, turned, scaled_stage, error_stage,
    send1, recv1, send2, recv2, send3, recv3, store_sem,
):
    blocks, _, width = x_ref.shape
    half = width // 2
    lanes = h_ref.shape[3]
    slabs = lanes // LANES
    rows = blocks * SUB
    me = lax.axis_index("row")
    far_first = sorted(range(1, peers), key=lambda d: (abs(d - peers // 2), d))
    others = [lax.rem(me + d, peers) for d in far_first]

    def remote(src, dst, send_sem, recv_sem, peer):
        return pltpu.make_async_remote_copy(
            src_ref=src, dst_ref=dst, send_sem=send_sem, recv_sem=recv_sem,
            device_id={"row": peer}, device_id_type=MESH,
        )

    def copy1(s, peer, land):
        return remote(out1.at[s, peer], in1.at[s, land], send1.at[s, peer], recv1.at[s, land], peer)

    def copy2(s, k, peer, land):
        return remote(
            out2.at[s, k, peer], in2.at[s, k, land], send2.at[s, k, peer], recv2.at[s, k, land], peer
        )

    def copy3(peer, land):
        return remote(peaks.at[me], peaks.at[land], send3.at[peer], recv3.at[land], peer)

    barrier = pltpu.get_barrier_semaphore()
    for peer in others:
        pl.semaphore_signal(barrier, inc=1, device_id={"row": peer}, device_id_type=MESH)
    pl.semaphore_wait(barrier, peers - 1)

    def column_side(peer, dst, place):
        def step(j, _):
            low = jnp.dot(x_ref[j, :, :half], h_ref[0, peer], preferred_element_type=jnp.float32)
            high = jnp.dot(x_ref[j, :, half:], h_ref[1, peer], preferred_element_type=jnp.float32)
            left = left_ref[j]
            for s, both in ((0, low + high), (1, low - high)):
                both = both * left
                parts = fold_rows([both[k * SUB:(k + 1) * SUB] for k in range(FOLD)])
                for k in range(FOLD):
                    dst[s, place, k, pl.ds(pl.multiple_of(j * SUB, SUB), SUB), :] = parts[k].astype(jnp.bfloat16)
            return 0

        lax.fori_loop(0, blocks, step, 0)

    for peer in others:
        column_side(peer, out1, peer)
        copy1(0, peer, me).start()
    for peer in others:
        copy1(1, peer, me).start()
    column_side(me, in1, me)

    def row_side(s, send):
        for peer in others:
            copy1(s, peer, peer).wait_recv()

        def step(k, peak):
            z = in1[s, :, k].reshape(peers * rows, lanes)
            r = jnp.dot(m_ref[...], z, preferred_element_type=jnp.float32)
            out2[s, k] = r.astype(jnp.bfloat16).reshape(peers, rows, lanes)
            if send:
                for peer in others:
                    copy2(s, k, peer, me).start()
            return jnp.maximum(peak, jnp.max(jnp.abs(r).reshape(-1, 8, lanes), axis=0))

        peak = lax.fori_loop(0, FOLD, step, jnp.zeros((8, lanes), jnp.float32))
        peaks[me, s] = jnp.broadcast_to(jnp.max(peak, axis=0, keepdims=True), (8, lanes))

    row_side(0, True)
    row_side(1, False)
    for peer in others:
        copy3(peer, me).start()

    def send_second(k, _):
        for peer in others:
            copy2(1, k, peer, me).start()
        return 0

    lax.fori_loop(0, FOLD, send_second, 0)

    def keep_own(k, _):
        for s in range(2):
            in2[s, k, me] = out2[s, k, me]
        return 0

    lax.fori_loop(0, FOLD, keep_own, 0)

    for peer in others:
        copy3(peer, peer).wait_recv()
    column_peak = jnp.concatenate([peaks[q, s, 0:1, :] for s in range(2) for q in range(peers)], axis=1)
    group = group_ref[...]
    column_scale = jnp.zeros_like(column_peak)
    group_scale = jnp.zeros((8, LANES), jnp.float32)
    lane = lax.broadcasted_iota(jnp.int32, (8, LANES), 1)
    for g in range(GROUPS):
        inside = group == g
        peak = jnp.maximum(jnp.max(jnp.where(inside, column_peak, 0.0), axis=1, keepdims=True), 1.0)
        column_scale = jnp.where(inside, 2.0 / peak, column_scale)
        group_scale = jnp.where(lane == g, peak * 0.5, group_scale)
    scale_ref[...] = group_scale
    sum_ref[...] = jnp.zeros_like(sum_ref)

    total_rows = peers * blocks * HB

    def stores(s, k, slot):
        return (
            pltpu.make_async_copy(
                scaled_stage.at[slot], scaled_ref.at[:, k, :, pl.ds(s * half, half)], store_sem.at[0, slot]
            ),
            pltpu.make_async_copy(
                error_stage.at[slot], error_ref.at[:, k, :, pl.ds(s * LANES, LANES)], store_sem.at[1, slot]
            ),
        )

    for s in range(2):
        scales = [
            column_scale[:, s * half + c * LANES:s * half + (c + 1) * LANES] for c in range(OCT)
        ]

        def lattice(k, _, s=s, scales=scales):
            slot = lax.rem(k, 2)
            for peer in others:
                copy2(s, k, peer, peer).wait_recv()

            if s:
                for copy in stores(s, k, slot):
                    copy.wait()
            else:

                @pl.when(k >= 2)
                def _():
                    for copy in stores(s, k, slot):
                        copy.wait()

            def tile(j, _):
                at = pl.ds(pl.multiple_of(j * SUB, SUB), SUB)
                square = near = low = size = most = least = None
                for c in range(OCT):
                    q, part = c // slabs, c % slabs
                    rotated = in2[s, k, q, at, part * LANES:(part + 1) * LANES].astype(jnp.float32)
                    value = rotated * scales[c]
                    turned[at, c * LANES:(c + 1) * LANES] = value.astype(jnp.bfloat16)
                    nearest = jnp.round(value)
                    offset = jnp.abs(value - nearest)
                    below = jnp.floor(value)
                    if c == 0:
                        square, near, low, size = offset * offset, nearest, below, offset
                        most = least = offset
                    else:
                        square, near, low = square + offset * offset, near + nearest, low + below
                        size = size + offset
                        most, least = jnp.maximum(most, offset), jnp.minimum(least, offset)
                odd = near - 2.0 * jnp.floor(near * 0.5) > 0.5
                whole = jnp.where(odd, square + (1.0 - 2.0 * most), square)
                shifted = square + (OCT * 0.25 - size)
                odd = low - 2.0 * jnp.floor(low * 0.5) > 0.5
                error = jnp.minimum(whole, jnp.where(odd, shifted + 2.0 * least, shifted))
                error_stage[slot, j] = error
                row = me * (blocks * HB) + j * HB + k * SUB + lax.broadcasted_iota(jnp.int32, (SUB, LANES), 0)
                weight = (1.0 + 4.0 * (row.astype(jnp.float32) + 0.5) / total_rows) / 3.0
                sum_ref[...] += error * weight
                return 0

            lax.fori_loop(0, blocks, tile, 0)
            natural = jnp.dot(turned[...], p_ref[...], preferred_element_type=jnp.float32)
            scaled_stage[slot] = natural.astype(jnp.bfloat16).reshape(blocks, SUB, half)
            for copy in stores(s, k, slot):
                copy.start()
            return 0

        lax.fori_loop(0, FOLD, lattice, 0)

    for slot in range(2):
        for copy in stores(1, slot, slot):
            copy.wait()
    for s in range(2):
        for peer in others:
            copy1(s, peer, me).wait_send()
    for peer in others:
        copy3(peer, me).wait_send()

    def drain(k, _):
        for s in range(2):
            for peer in others:
                copy2(s, k, peer, me).wait_send()
        return 0

    lax.fori_loop(0, FOLD, drain, 0)


def body(weights, left_bits, right_bits, groups):
    _, local_rows, width = weights.shape
    peers = lax.axis_size("row")
    experts = lax.axis_size("expert")
    blocks = local_rows // HB
    half = width // 2
    lanes = half // peers
    rows = blocks * SUB
    scale = 1.0 / math.sqrt(width * HB)
    h = column_matrix(right_bits, peers, half, scale)
    left = (2 * left_bits - 1).astype(jnp.float32).reshape(blocks, HB, 1)
    ordered = groups.reshape(2, LANES, OCT).transpose(0, 2, 1).reshape(1, width)
    vmem = pl.BlockSpec(memory_space=pltpu.VMEM)
    hbm = pl.BlockSpec(memory_space=pl.ANY)
    dma = pltpu.SemaphoreType.DMA
    scaled, errors, group_scale, sums = pl.pallas_call(
        functools.partial(kernel, peers),
        out_shape=(
            jax.ShapeDtypeStruct((blocks, FOLD, SUB, width), jnp.bfloat16),
            jax.ShapeDtypeStruct((blocks, FOLD, SUB, width // OCT), jnp.float32),
            jax.ShapeDtypeStruct((8, LANES), jnp.float32),
            jax.ShapeDtypeStruct((SUB, LANES), jnp.float32),
        ),
        in_specs=[vmem] * 6,
        out_specs=(hbm, hbm, vmem, vmem),
        scratch_shapes=[
            pltpu.VMEM((2, peers, FOLD, rows, lanes), jnp.bfloat16),
            pltpu.VMEM((2, peers, FOLD, rows, lanes), jnp.bfloat16),
            pltpu.VMEM((2, FOLD, peers, rows, lanes), jnp.bfloat16),
            pltpu.VMEM((2, FOLD, peers, rows, lanes), jnp.bfloat16),
            pltpu.VMEM((peers, 2, 8, lanes), jnp.float32),
            pltpu.VMEM((rows, half), jnp.bfloat16),
            pltpu.VMEM((2, blocks, SUB, half), jnp.bfloat16),
            pltpu.VMEM((2, blocks, SUB, LANES), jnp.float32),
            dma((2, peers)),
            dma((2, peers)),
            dma((2, FOLD, peers)),
            dma((2, FOLD, peers)),
            dma((peers,)),
            dma((peers,)),
            dma((2, 2)),
        ],
        compiler_params=pltpu.CompilerParams(
            collective_id=0, has_side_effects=True, vmem_limit_bytes=60 * 2**20
        ),
    )(weights.reshape(blocks, HB, width), left, ordered, h, row_matrix(), order_matrix(half))
    partial_error = jnp.sum(sums) / (local_rows * peers * width // OCT)
    mine = lax.axis_index("expert")
    spread = jnp.where(jnp.arange(experts) == mine, partial_error, 0.0)
    every = lax.psum(spread, ("row", "expert"))
    expert_error = lax.dynamic_slice_in_dim(every, mine, 1)
    return (
        scaled.reshape(1, local_rows, width),
        errors.reshape(1, local_rows, width // OCT),
        group_scale[:1, :GROUPS],
        expert_error,
        jnp.sum(every) / experts,
    )


def solution(mesh):
    placed = (P("expert", "row", None), P("expert", "row"), P("expert", None), P("expert", None))
    return jax.shard_map(
        body,
        mesh=mesh,
        in_specs=placed,
        out_specs=(
            P("expert", "row", None),
            P("expert", "row", None),
            P("expert", None),
            P("expert"),
            P(),
        ),
        check_vma=False,
    )
```

time: 743 us -> 434 us (0.58); the launches traced: 734 us -> 433 us
  waiting for transfers between devices: 496 us -> 0 us
  Pallas kernels: 0 us -> 335 us
  matrix products: 81.6 us -> 0 us
  other arithmetic: 53.5 us -> 25.8 us
  local copies, waits for them, and re-layouts: 53.9 us -> 28.1 us
  between operations: 16.7 us -> 3.16 us
  blocking collectives: 32.6 us -> 41.6 us
    all_gather x1 -> x0, waiting for transfers between devices: 496 us -> none  [body(): lax.all_gather(blocked, 'row', axis=1, tiled=True)]
    pallas_call x0 -> x1, Pallas kernels: none -> 335 us  [body(): pl.pallas_call(functools.partial(kernel, peers), out_shape=(jax.ShapeDtyp...]
    dot_general x4 -> x0, matrix products: 81.6 us -> none  [the longest x1 31.9 us: body(): jnp.einsum('ij,ejbf->eibf', own_matrix, lax.all_gather(blocked, 'row', ax...]
    reduce_sum x3 -> x2, other arithmetic: 35.9 us -> 1.9 us  [the longest x1 1.3 us: body(): partial_error = jnp.sum(sums) / (local_rows * peers * width // OCT)]
    psum x2 -> x1, blocking collectives: 23.7 us -> 41.6 us  [body(): every = lax.psum(spread, ('row', 'expert'))]
    div x1 -> x0, local copies, waits for them, and re-layouts: 17.6 us -> none  [row_transform(): return turned / math.sqrt(HB)]
    reshape x1 -> x2, local copies, waits for them, and re-layouts: 16.9 us -> 1.83 us  [the longest x1 1.74 us: body(): left = (2 * left_bits - 1).astype(jnp.float32).reshape(blocks, HB, 1)]
    convert_element_type x3 -> x7, other arithmetic: 11.8 us -> 22.5 us  [the longest x1 11.4 us: column_matrix(): return full.astype(jnp.bfloat16).reshape(2, peers, half, slabs * LANES)]
  transfers between devices with their start and end apart: 1 -> 0, of which waited for: 1 -> 0; matrix products, arithmetic and copies ran while one was open for 0% -> 0% of each run, Pallas kernels for 0% -> 0%
where the time goes in v1:
time: 434 us; the launch traced here: 433 us
  Pallas kernels  335 us (77%)
  blocking collectives  41.6 us (10%)
  local copies, waits for them, and re-layouts  28.1 us (6%)
  other arithmetic  25.8 us (6%)
    pallas_call x1, Pallas kernels, body(): pl.pallas_call(functools.partial(kernel, peers), out_shape=(jax.ShapeDtyp...  335 us
    psum x1, blocking collectives, body(): every = lax.psum(spread, ('row', 'expert'))  41.6 us
    convert_element_type x1, local copies, waits for them, and re-layouts, row_matrix(): return full.reshape(size, size).astype(jnp.bfloat16)  14.4 us
    convert_element_type x1, other arithmetic, column_matrix(): return full.astype(jnp.bfloat16).reshape(2, peers, half, slabs * LANES)  11.4 us
    unnamed x5, local copies, waits for them, and re-layouts  9.27 us

profile of v1, /device:TPU:0, one launch (start us, length us, event | category | flops | bytes accessed | tf_op | source)
XLA Modules:
  0.0 433.5 jit_solution(11806367811332597275)
XLA Ops:
  0.6 0.7 convert_reduce_fusion.1
  1.4 1.7 reshape.124.left_ref
  3.1 0.5 broadcast.226
  3.6 1.4 reduce.9
  5.0 0.1 reshape.120
  5.1 0.7 copy.10
  5.7 0.7 convert_reduce_fusion
  6.5 11.4 %multiply_convert_fusion.1.h_ref = bf16[2,4,1024,256]{3,2,1,0:T(8,128)(2,1)} fusion(f32[2,1024]{1,0:T(2,128)S(1)} %mul.136, s32[256]{0:T(256)S(1)} %get-tuple-element.13, s32[4]{0:T(128)S(1)} %iota_multiply_fusion, s32[256]{0:T(256)S(1)} %get-tuple-element.14), kind=kLoop, calls=%fused_computation.1 | loop fusion | flops 79691776 | bytes 4204560 | tf_op jit(solution)/shard_map/convert_element_type | solution.py:43
  18.0 0.1 fusion.1
  18.1 6.7 %multiply_convert_fusion = bf16[56,16,56,16]{3,2,1,0:T(8,128)(2,1)} fusion(f32[16,16]{1,0:T(8,128)S(1)} %subtract_convert_fusion, f32[56,56]{1,0:T(8,128)S(1)} %fusion.1), kind=kLoop, calls=%fused_computation | loop fusion | flops 1605632 | bytes 1619200 | tf_op jit(solution)/shard_map/convert_element_type | solution.py:52
  24.9 14.4 %convert_element_type.51.m_ref = bf16[896,896]{1,0:T(8,128)(2,1)} reshape(bf16[56,16,56,16]{3,2,1,0:T(8,128)(2,1)} %multiply_convert_fusion) | data formatting | bytes 3211264 | tf_op jit(solution)/shard_map/convert_element_type | solution.py:52
  39.3 2.7 fusion.p_ref
  42.0 334.8 %shard_map.83 = (bf16[14,8,16,2048]{3,2,1,0:T(8,128)(2,1)}, f32[14,8,16,256]{3,2,1,0:T(8,128)}, f32[8,128]{1,0:T(8,128)}, f32[16,128]{1,0:T(8,128)}) custom-call(bf16[14,128,2048]{2,1,0:T(8,128)(2,1)} %bitcast.11, f32[14,128,1]{2,1,0:T(8,128)} %reshape.124.left_ref, s32[1,2048]{1,0:T(1,128)} %bitcast.15, ...), custom_call_target="tpu_custom_call" | custom-call | tf_op jit(solution)/shard_map/pallas_call | solution.py:285
  376.8 0.0 copy-start
  376.8 1.3 slice.3
  378.2 1.3 reduce_sum.18
  380.1 41.6 %psum.7 = f32[8]{0:T(128)S(1)} all-reduce(f32[8]{0:T(128)S(1)} %compare_select_fusion), channel_id=1, replica_groups=mesh['expert'=8,'row'=4] {'row','expert'}, use_global_device_ids=true, to_apply=%region_1.2 | all-reduce | flops 8 | bytes 64 | tf_op jit(solution)/shard_map/psum | solution.py:319
  421.7 0.6 dynamic_slice.3
  422.3 0.6 reduce_sum.19
  423.6 7.5 %copy.14 = bf16[1,1792,2048]{2,1,0:T(8,128)(2,1)} copy(bf16[1,1792,2048]{2,1,0:T(8,128)(2,1)} %bitcast.12) | data formatting | bytes 14680064
  431.1 0.0 copy-done
  431.1 1.2 copy.15
  (11 shorter events, 0.1 us)
Async XLA Ops:
  376.8 54.3 %copy-start = (f32[14,8,16,256]{3,2,1,0:T(8,128)S(1)}, f32[14,8,16,256]{3,2,1,0:T(8,128)}, u32[]{:S(2)}) copy-start(f32[14,8,16,256]{3,2,1,0:T(8,128)} %get-tuple-element.10) | copy-start | bytes 5505028

commit v2 on v1

--- a/solution.py
+++ b/solution.py
@@ -19,10 +19,18 @@
 
 
 def signs(common, bits):
-    parity = common & 1
-    for bit_pos in range(1, bits):
-        parity = parity + ((common >> bit_pos) & 1)
-    return (1 - 2 * (parity & 1)).astype(jnp.float32)
+    for shift in (4, 2, 1):
+        if shift < bits:
+            common = common ^ (common >> shift)
+    return (1 - 2 * (common & 1)).astype(jnp.float32)
+
+
+def iota(shape, dim):
+    return lax.broadcasted_iota(jnp.int32, shape, dim)
+
+
+def down(row):
+    return jnp.broadcast_to(row, (LANES, LANES)).T
 
 
 def cosine_block(order):
@@ -32,31 +40,64 @@
     return jnp.where(first == 0.0, table * math.sqrt(0.5), table)
 
 
-def column_matrix(right_bits, peers, half, scale):
-    slabs = OCT // peers
-    shape = (2, peers, half, slabs, LANES)
-    row = lax.broadcasted_iota(jnp.int32, shape, 2)
-    slab = lax.broadcasted_iota(jnp.int32, shape, 1) * slabs + lax.broadcasted_iota(jnp.int32, shape, 3)
-    col = lax.broadcasted_iota(jnp.int32, shape, 4) * OCT + slab
-    sign = (2 * right_bits - 1).astype(jnp.float32).reshape(2, 1, half, 1, 1)
-    full = signs(row & col, half.bit_length() - 1) * sign * scale
-    return full.astype(jnp.bfloat16).reshape(2, peers, half, slabs * LANES)
-
-
-def row_matrix():
-    cosine = cosine_block(BLOCKS).astype(jnp.bfloat16).astype(jnp.float32)
-    index = jnp.arange(SUB, dtype=jnp.int32)
-    small = signs(index[:, None] & index[None, :], SUB.bit_length() - 1)
-    size = BLOCKS * SUB
-    full = cosine[:, None, :, None] * small[None, :, None, :]
-    return full.reshape(size, size).astype(jnp.bfloat16)
-
-
-def order_matrix(half):
-    source = lax.broadcasted_iota(jnp.int32, (half, half), 0)
-    target = lax.broadcasted_iota(jnp.int32, (half, half), 1)
-    wanted = (source % LANES) * OCT + source // LANES
-    return (wanted == target).astype(jnp.bfloat16)
+def build_column(right_ref, h_ref, scale):
+    slabs = h_ref.shape[3] // LANES
+    half = h_ref.shape[2]
+    square = (LANES, LANES)
+    octave = [signs((iota(square, 0) & (OCT - 1)) & s, 3) for s in range(OCT)]
+
+    def step(u, _):
+        at = pl.ds(pl.multiple_of(u * LANES, LANES), LANES)
+        outer = signs(((u * LANES + iota(square, 0)) >> 3) & iota(square, 1), 7)
+        for side in range(2):
+            bits = right_ref[:, pl.ds(pl.multiple_of(side * half + u * LANES, LANES), LANES)]
+            part = outer * down((2 * bits - 1).astype(jnp.float32) * scale)
+            for s in range(OCT):
+                q, slab = s // slabs, s % slabs
+                h_ref[side, q, at, slab * LANES:(slab + 1) * LANES] = (part * octave[s]).astype(jnp.bfloat16)
+        return 0
+
+    lax.fori_loop(0, half // LANES, step, 0)
+
+
+def build_left(left_ref, left):
+    def step(j, _):
+        bits = left_ref[:, pl.ds(pl.multiple_of(j * HB, HB), HB)]
+        left[j] = down((2 * bits - 1).astype(jnp.float32))
+        return 0
+
+    lax.fori_loop(0, left.shape[0], step, 0)
+
+
+def build_row(cosine_ref, m_ref):
+    size = m_ref.shape[0]
+    spread = (iota((size, BLOCKS), 0) // SUB == iota((size, BLOCKS), 1)).astype(jnp.float32).astype(jnp.bfloat16)
+    chunk = size // 7
+
+    def step(u, _):
+        at = pl.multiple_of(u * chunk, chunk)
+        here = ((at + iota((chunk, BLOCKS), 0)) // SUB == iota((chunk, BLOCKS), 1)).astype(jnp.float32)
+        rows = jnp.dot(here.astype(jnp.bfloat16), cosine_ref[...], preferred_element_type=jnp.float32)
+        full = lax.dot_general(
+            rows.astype(jnp.bfloat16), spread, (((1,), (1,)), ((), ())), preferred_element_type=jnp.float32
+        )
+        small = signs((iota((chunk, size), 0) & iota((chunk, size), 1)) & (SUB - 1), 4)
+        m_ref[pl.ds(at, chunk), :] = (full * small).astype(jnp.bfloat16)
+        return 0
+
+    lax.fori_loop(0, 7, step, 0)
+
+
+def build_order(p_ref):
+    half = p_ref.shape[0]
+
+    def step(s, _):
+        wanted = iota((LANES, half), 0) * OCT + s
+        hit = (wanted == iota((LANES, half), 1)).astype(jnp.float32)
+        p_ref[pl.ds(pl.multiple_of(s * LANES, LANES), LANES), :] = hit.astype(jnp.bfloat16)
+        return 0
+
+    lax.fori_loop(0, OCT, step, 0)
 
 
 def fold_rows(parts):
@@ -72,10 +113,11 @@
 
 
 def kernel(
-    peers, x_ref, left_ref, group_ref, h_ref, m_ref, p_ref,
-    scaled_ref, error_ref, scale_ref, sum_ref,
-    out1, in1, out2, in2, peaks, turned, scaled_stage, error_stage,
-    send1, recv1, send2, recv2, send3, recv3, store_sem,
+    peers, experts, x_hbm, left_ref, right_ref, group_ref, cosine_ref,
+    scaled_ref, error_ref, scale_ref, mean_ref, total_ref,
+    x_ref, left, h_ref, m_ref, p_ref, out1, in1, out2, in2, peaks, turned, scaled_stage, error_stage,
+    sum_ref, row_sums, expert_sums,
+    send1, recv1, send2, recv2, send3, recv3, send4, recv4, send5, recv5, store_sem, load_sem,
 ):
     blocks, _, width = x_ref.shape
     half = width // 2
@@ -83,8 +125,12 @@
     slabs = lanes // LANES
     rows = blocks * SUB
     me = lax.axis_index("row")
+    mine = lax.axis_index("expert")
+    load = pltpu.make_async_copy(x_hbm, x_ref, load_sem)
+    load.start()
     far_first = sorted(range(1, peers), key=lambda d: (abs(d - peers // 2), d))
     others = [lax.rem(me + d, peers) for d in far_first]
+    elsewhere = [lax.rem(mine + d, experts) for d in range(1, experts)]
 
     def remote(src, dst, send_sem, recv_sem, peer):
         return pltpu.make_async_remote_copy(
@@ -103,18 +149,32 @@
     def copy3(peer, land):
         return remote(peaks.at[me], peaks.at[land], send3.at[peer], recv3.at[land], peer)
 
+    def copy4(peer, land):
+        return remote(row_sums.at[me], row_sums.at[land], send4.at[peer], recv4.at[land], peer)
+
+    def copy5(peer, land):
+        return pltpu.make_async_remote_copy(
+            src_ref=expert_sums.at[mine], dst_ref=expert_sums.at[land],
+            send_sem=send5.at[peer], recv_sem=recv5.at[land],
+            device_id={"expert": peer}, device_id_type=MESH,
+        )
+
     barrier = pltpu.get_barrier_semaphore()
     for peer in others:
         pl.semaphore_signal(barrier, inc=1, device_id={"row": peer}, device_id_type=MESH)
-    pl.semaphore_wait(barrier, peers - 1)
+    for peer in elsewhere:
+        pl.semaphore_signal(barrier, inc=1, device_id={"expert": peer}, device_id_type=MESH)
+    build_column(right_ref, h_ref, 1.0 / math.sqrt(width * HB))
+    build_left(left_ref, left)
+    load.wait()
 
     def column_side(peer, dst, place):
         def step(j, _):
             low = jnp.dot(x_ref[j, :, :half], h_ref[0, peer], preferred_element_type=jnp.float32)
             high = jnp.dot(x_ref[j, :, half:], h_ref[1, peer], preferred_element_type=jnp.float32)
-            left = left_ref[j]
+            sign = jnp.concatenate([left[j]] * slabs, axis=1)
             for s, both in ((0, low + high), (1, low - high)):
-                both = both * left
+                both = both * sign
                 parts = fold_rows([both[k * SUB:(k + 1) * SUB] for k in range(FOLD)])
                 for k in range(FOLD):
                     dst[s, place, k, pl.ds(pl.multiple_of(j * SUB, SUB), SUB), :] = parts[k].astype(jnp.bfloat16)
@@ -122,12 +182,16 @@
 
         lax.fori_loop(0, blocks, step, 0)
 
-    for peer in others:
+    for step, peer in enumerate(others):
         column_side(peer, out1, peer)
+        if step == 0:
+            pl.semaphore_wait(barrier, peers + experts - 2)
         copy1(0, peer, me).start()
     for peer in others:
         copy1(1, peer, me).start()
     column_side(me, in1, me)
+    build_row(cosine_ref, m_ref)
+    build_order(p_ref)
 
     def row_side(s, send):
         for peer in others:
@@ -167,16 +231,23 @@
     for peer in others:
         copy3(peer, peer).wait_recv()
     column_peak = jnp.concatenate([peaks[q, s, 0:1, :] for s in range(2) for q in range(peers)], axis=1)
-    group = group_ref[...]
+    spread = jnp.broadcast_to(group_ref[...], (8, width)).astype(jnp.float32).astype(jnp.bfloat16)
+    group = jnp.concatenate([
+        lax.dot_general(
+            spread[:, s * half:(s + 1) * half], p_ref[...], (((1,), (1,)), ((), ())),
+            preferred_element_type=jnp.float32,
+        )[:1]
+        for s in range(2)
+    ], axis=1)
     column_scale = jnp.zeros_like(column_peak)
     group_scale = jnp.zeros((8, LANES), jnp.float32)
     lane = lax.broadcasted_iota(jnp.int32, (8, LANES), 1)
     for g in range(GROUPS):
-        inside = group == g
+        inside = group == float(g)
         peak = jnp.maximum(jnp.max(jnp.where(inside, column_peak, 0.0), axis=1, keepdims=True), 1.0)
         column_scale = jnp.where(inside, 2.0 / peak, column_scale)
         group_scale = jnp.where(lane == g, peak * 0.5, group_scale)
-    scale_ref[...] = group_scale
+    scale_ref[...] = group_scale[:1, :GROUPS]
     sum_ref[...] = jnp.zeros_like(sum_ref)
 
     total_rows = peers * blocks * HB
@@ -249,6 +320,26 @@
 
         lax.fori_loop(0, FOLD, lattice, 0)
 
+    part = jnp.sum(jnp.sum(sum_ref[...], axis=0, keepdims=True), axis=1, keepdims=True)
+    row_sums[me] = jnp.broadcast_to(part / (total_rows * width // OCT), (8, LANES))
+    for peer in others:
+        copy4(peer, me).start()
+    for peer in others:
+        copy4(peer, peer).wait_recv()
+    mean = row_sums[0]
+    for q in range(1, peers):
+        mean = mean + row_sums[q]
+    expert_sums[mine] = mean
+    for peer in elsewhere:
+        copy5(peer, mine).start()
+    for peer in elsewhere:
+        copy5(peer, peer).wait_recv()
+    total = expert_sums[0]
+    for e in range(1, experts):
+        total = total + expert_sums[e]
+    mean_ref[0] = jnp.max(mean)
+    total_ref[0] = jnp.max(total / experts)
+
     for slot in range(2):
         for copy in stores(1, slot, slot):
             copy.wait()
@@ -257,6 +348,9 @@
             copy1(s, peer, me).wait_send()
     for peer in others:
         copy3(peer, me).wait_send()
+        copy4(peer, me).wait_send()
+    for peer in elsewhere:
+        copy5(peer, mine).wait_send()
 
     def drain(k, _):
         for s in range(2):
@@ -275,24 +369,28 @@
     half = width // 2
     lanes = half // peers
     rows = blocks * SUB
-    scale = 1.0 / math.sqrt(width * HB)
-    h = column_matrix(right_bits, peers, half, scale)
-    left = (2 * left_bits - 1).astype(jnp.float32).reshape(blocks, HB, 1)
-    ordered = groups.reshape(2, LANES, OCT).transpose(0, 2, 1).reshape(1, width)
+    cosine = cosine_block(BLOCKS).astype(jnp.bfloat16)
     vmem = pl.BlockSpec(memory_space=pltpu.VMEM)
     hbm = pl.BlockSpec(memory_space=pl.ANY)
     dma = pltpu.SemaphoreType.DMA
-    scaled, errors, group_scale, sums = pl.pallas_call(
-        functools.partial(kernel, peers),
+    smem = pl.BlockSpec(memory_space=pltpu.SMEM)
+    scaled, errors, group_scale, mean, total = pl.pallas_call(
+        functools.partial(kernel, peers, experts),
         out_shape=(
             jax.ShapeDtypeStruct((blocks, FOLD, SUB, width), jnp.bfloat16),
             jax.ShapeDtypeStruct((blocks, FOLD, SUB, width // OCT), jnp.float32),
-            jax.ShapeDtypeStruct((8, LANES), jnp.float32),
-            jax.ShapeDtypeStruct((SUB, LANES), jnp.float32),
+            jax.ShapeDtypeStruct((1, GROUPS), jnp.float32),
+            jax.ShapeDtypeStruct((1,), jnp.float32),
+            jax.ShapeDtypeStruct((1,), jnp.float32),
         ),
-        in_specs=[vmem] * 6,
-        out_specs=(hbm, hbm, vmem, vmem),
+        in_specs=[hbm] + [vmem] * 4,
+        out_specs=(hbm, hbm, vmem, smem, smem),
         scratch_shapes=[
+            pltpu.VMEM((blocks, HB, width), jnp.bfloat16),
+            pltpu.VMEM((blocks, HB, LANES), jnp.float32),
+            pltpu.VMEM((2, peers, half, lanes), jnp.bfloat16),
+            pltpu.VMEM((BLOCKS * SUB, BLOCKS * SUB), jnp.bfloat16),
+            pltpu.VMEM((half, half), jnp.bfloat16),
             pltpu.VMEM((2, peers, FOLD, rows, lanes), jnp.bfloat16),
             pltpu.VMEM((2, peers, FOLD, rows, lanes), jnp.bfloat16),
             pltpu.VMEM((2, FOLD, peers, rows, lanes), jnp.bfloat16),
@@ -301,29 +399,32 @@
             pltpu.VMEM((rows, half), jnp.bfloat16),
             pltpu.VMEM((2, blocks, SUB, half), jnp.bfloat16),
             pltpu.VMEM((2, blocks, SUB, LANES), jnp.float32),
+            pltpu.VMEM((SUB, LANES), jnp.float32),
+            pltpu.VMEM((peers, 8, LANES), jnp.float32),
+            pltpu.VMEM((experts, 8, LANES), jnp.float32),
             dma((2, peers)),
             dma((2, peers)),
             dma((2, FOLD, peers)),
             dma((2, FOLD, peers)),
             dma((peers,)),
             dma((peers,)),
+            dma((peers,)),
+            dma((peers,)),
+            dma((experts,)),
+            dma((experts,)),
             dma((2, 2)),
+            dma,
         ],
         compiler_params=pltpu.CompilerParams(
             collective_id=0, has_side_effects=True, vmem_limit_bytes=60 * 2**20
         ),
-    )(weights.reshape(blocks, HB, width), left, ordered, h, row_matrix(), order_matrix(half))
-    partial_error = jnp.sum(sums) / (local_rows * peers * width // OCT)
-    mine = lax.axis_index("expert")
-    spread = jnp.where(jnp.arange(experts) == mine, partial_error, 0.0)
-    every = lax.psum(spread, ("row", "expert"))
-    expert_error = lax.dynamic_slice_in_dim(every, mine, 1)
+    )(weights.reshape(blocks, HB, width), left_bits, right_bits, groups, cosine)
     return (
         scaled.reshape(1, local_rows, width),
         errors.reshape(1, local_rows, width // OCT),
-        group_scale[:1, :GROUPS],
-        expert_error,
-        jnp.sum(every) / experts,
+        group_scale,
+        mean,
+        total.reshape(()),
     )
 
 

time: 434 us -> 354 us (0.82)
  blocking collectives: 41.6 us -> 0 us
  other arithmetic: 25.8 us -> 0.75 us
  local copies, waits for them, and re-layouts: 28.1 us -> 9.4 us
  Pallas kernels: 335 us -> 340 us
    psum x1 -> x0, blocking collectives: 41.6 us -> none  [body(): every = lax.psum(spread, ('row', 'expert'))]
    convert_element_type x7 -> x1, other arithmetic: 22.5 us -> 0.73 us  [body(): cosine = cosine_block(BLOCKS).astype(jnp.bfloat16)]
    convert_element_type x1 -> x0, local copies, waits for them, and re-layouts: 14.4 us -> none  [row_matrix(): return full.reshape(size, size).astype(jnp.bfloat16)]
    pallas_call x1, Pallas kernels: 335 us -> 340 us  [body(): pl.pallas_call(functools.partial(kernel, peers, experts), out_shape=(jax....]
    unnamed x5 -> x7, local copies, waits for them, and re-layouts: 9.27 us -> 9.4 us
where the time goes in v2:
time: 354 us
  Pallas kernels  340 us (96%)
  local copies, waits for them, and re-layouts  9.4 us (3%)
  between operations  4.11 us (1%)
    pallas_call x1, Pallas kernels, body(): pl.pallas_call(functools.partial(kernel, peers, experts), out_shape=(jax....  340 us
    unnamed x7, local copies, waits for them, and re-layouts  9.4 us

profile of v2, /device:TPU:0, one launch (start us, length us, event | category | flops | bytes accessed | tf_op | source)
XLA Modules:
  0.0 354.1 jit_solution(13854625831723613317)
XLA Ops:
  0.7 0.7 select_convert_fusion.cosine_ref
  1.4 339.8 %shard_map.83 = (bf16[14,8,16,2048]{3,2,1,0:T(8,128)(2,1)}, f32[14,8,16,256]{3,2,1,0:T(8,128)}, f32[1,16]{1,0:T(1,128)}, f32[1]{0:T(128)}, f32[1]{0:T(128)}) custom-call(bf16[14,128,2048]{2,1,0:T(8,128)(2,1)} %bitcast.4, s32[1,1792]{1,0:T(1,128)} %left_ref.1, s32[1,2048]{1,0:T(1,128)} %right_ref.1, s32[1,2048]{1,0:T(1,128)} %group_ref.1, ...), custom_call_target="tpu_custom_call" | custom-call | tf_op jit(solution)/shard_map/pallas_call | solution.py:377
  341.2 0.0 copy-start
  341.2 0.0 copy-start.1
  341.3 7.7 %copy.14 = bf16[1,1792,2048]{2,1,0:T(8,128)(2,1)} copy(bf16[1,1792,2048]{2,1,0:T(8,128)(2,1)} %bitcast.5) | data formatting | bytes 14680064
  348.9 0.0 copy-done
  348.9 1.2 copy.15
  350.1 0.0 copy-done.1
  350.1 0.5 copy.16
  (2 shorter events, 0.0 us)
Async XLA Ops:
  341.2 7.7 %copy-start = (f32[14,8,16,256]{3,2,1,0:T(8,128)S(1)}, f32[14,8,16,256]{3,2,1,0:T(8,128)}, u32[]{:S(2)}) copy-start(f32[14,8,16,256]{3,2,1,0:T(8,128)} %get-tuple-element.11) | copy-start | bytes 5505028
  341.2 8.9 %copy-start.1 = (f32[1,16]{1,0:T(1,128)S(1)}, f32[1,16]{1,0:T(1,128)}, u32[]{:S(2)}) copy-start(f32[1,16]{1,0:T(1,128)} %get-tuple-element.22) | copy-start | bytes 196

commit v3 on v2

--- a/solution.py
+++ b/solution.py
@@ -115,9 +115,9 @@
 def kernel(
     peers, experts, x_hbm, left_ref, right_ref, group_ref, cosine_ref,
     scaled_ref, error_ref, scale_ref, mean_ref, total_ref,
-    x_ref, left, h_ref, m_ref, p_ref, out1, in1, out2, in2, peaks, turned, scaled_stage, error_stage,
+    x_ref, left, h_ref, m_ref, p_ref, out1, in1, out2, in2, peaks, turned,
     sum_ref, row_sums, expert_sums,
-    send1, recv1, send2, recv2, send3, recv3, send4, recv4, send5, recv5, store_sem, load_sem,
+    send1, recv1, send2, recv2, send3, recv3, send4, recv4, send5, recv5, load_sem,
 ):
     blocks, _, width = x_ref.shape
     half = width // 2
@@ -252,35 +252,14 @@
 
     total_rows = peers * blocks * HB
 
-    def stores(s, k, slot):
-        return (
-            pltpu.make_async_copy(
-                scaled_stage.at[slot], scaled_ref.at[:, k, :, pl.ds(s * half, half)], store_sem.at[0, slot]
-            ),
-            pltpu.make_async_copy(
-                error_stage.at[slot], error_ref.at[:, k, :, pl.ds(s * LANES, LANES)], store_sem.at[1, slot]
-            ),
-        )
-
     for s in range(2):
         scales = [
             column_scale[:, s * half + c * LANES:s * half + (c + 1) * LANES] for c in range(OCT)
         ]
 
         def lattice(k, _, s=s, scales=scales):
-            slot = lax.rem(k, 2)
             for peer in others:
                 copy2(s, k, peer, peer).wait_recv()
-
-            if s:
-                for copy in stores(s, k, slot):
-                    copy.wait()
-            else:
-
-                @pl.when(k >= 2)
-                def _():
-                    for copy in stores(s, k, slot):
-                        copy.wait()
 
             def tile(j, _):
                 at = pl.ds(pl.multiple_of(j * SUB, SUB), SUB)
@@ -305,7 +284,7 @@
                 shifted = square + (OCT * 0.25 - size)
                 odd = low - 2.0 * jnp.floor(low * 0.5) > 0.5
                 error = jnp.minimum(whole, jnp.where(odd, shifted + 2.0 * least, shifted))
-                error_stage[slot, j] = error
+                error_ref[j, k, :, s * LANES:(s + 1) * LANES] = error
                 row = me * (blocks * HB) + j * HB + k * SUB + lax.broadcasted_iota(jnp.int32, (SUB, LANES), 0)
                 weight = (1.0 + 4.0 * (row.astype(jnp.float32) + 0.5) / total_rows) / 3.0
                 sum_ref[...] += error * weight
@@ -313,9 +292,7 @@
 
             lax.fori_loop(0, blocks, tile, 0)
             natural = jnp.dot(turned[...], p_ref[...], preferred_element_type=jnp.float32)
-            scaled_stage[slot] = natural.astype(jnp.bfloat16).reshape(blocks, SUB, half)
-            for copy in stores(s, k, slot):
-                copy.start()
+            scaled_ref[:, k, :, s * half:(s + 1) * half] = natural.astype(jnp.bfloat16).reshape(blocks, SUB, half)
             return 0
 
         lax.fori_loop(0, FOLD, lattice, 0)
@@ -340,9 +317,6 @@
     mean_ref[0] = jnp.max(mean)
     total_ref[0] = jnp.max(total / experts)
 
-    for slot in range(2):
-        for copy in stores(1, slot, slot):
-            copy.wait()
     for s in range(2):
         for peer in others:
             copy1(s, peer, me).wait_send()
@@ -359,6 +333,31 @@
         return 0
 
     lax.fori_loop(0, FOLD, drain, 0)
+
+
+def put_kernel(scaled_ref, error_ref, scaled_out, error_out, sems):
+    copies = (
+        pltpu.make_async_copy(scaled_ref, scaled_out, sems.at[0]),
+        pltpu.make_async_copy(error_ref, error_out, sems.at[1]),
+    )
+    for copy in copies:
+        copy.start()
+    for copy in copies:
+        copy.wait()
+
+
+def put(scaled, errors):
+    return pl.pallas_call(
+        put_kernel,
+        out_shape=(
+            jax.ShapeDtypeStruct(scaled.shape, scaled.dtype),
+            jax.ShapeDtypeStruct(errors.shape, errors.dtype),
+        ),
+        in_specs=[pl.BlockSpec(memory_space=pltpu.VMEM)] * 2,
+        out_specs=[pl.BlockSpec(memory_space=pl.ANY)] * 2,
+        scratch_shapes=[pltpu.SemaphoreType.DMA((2,))],
+        compiler_params=pltpu.CompilerParams(vmem_limit_bytes=16 * 2**20),
+    )(scaled, errors)
 
 
 def body(weights, left_bits, right_bits, groups):
@@ -377,14 +376,14 @@
     scaled, errors, group_scale, mean, total = pl.pallas_call(
         functools.partial(kernel, peers, experts),
         out_shape=(
-            jax.ShapeDtypeStruct((blocks, FOLD, SUB, width), jnp.bfloat16),
-            jax.ShapeDtypeStruct((blocks, FOLD, SUB, width // OCT), jnp.float32),
+            pltpu.VMEM((blocks, FOLD, SUB, width), jnp.bfloat16),
+            pltpu.VMEM((blocks, FOLD, SUB, width // OCT), jnp.float32),
             jax.ShapeDtypeStruct((1, GROUPS), jnp.float32),
             jax.ShapeDtypeStruct((1,), jnp.float32),
             jax.ShapeDtypeStruct((1,), jnp.float32),
         ),
         in_specs=[hbm] + [vmem] * 4,
-        out_specs=(hbm, hbm, vmem, smem, smem),
+        out_specs=(vmem, vmem, vmem, smem, smem),
         scratch_shapes=[
             pltpu.VMEM((blocks, HB, width), jnp.bfloat16),
             pltpu.VMEM((blocks, HB, LANES), jnp.float32),
@@ -397,8 +396,6 @@
             pltpu.VMEM((2, FOLD, peers, rows, lanes), jnp.bfloat16),
             pltpu.VMEM((peers, 2, 8, lanes), jnp.float32),
             pltpu.VMEM((rows, half), jnp.bfloat16),
-            pltpu.VMEM((2, blocks, SUB, half), jnp.bfloat16),
-            pltpu.VMEM((2, blocks, SUB, LANES), jnp.float32),
             pltpu.VMEM((SUB, LANES), jnp.float32),
             pltpu.VMEM((peers, 8, LANES), jnp.float32),
             pltpu.VMEM((experts, 8, LANES), jnp.float32),
@@ -412,13 +409,13 @@
             dma((peers,)),
             dma((experts,)),
             dma((experts,)),
-            dma((2, 2)),
             dma,
         ],
         compiler_params=pltpu.CompilerParams(
-            collective_id=0, has_side_effects=True, vmem_limit_bytes=60 * 2**20
+            collective_id=0, has_side_effects=True, vmem_limit_bytes=48 * 2**20
         ),
     )(weights.reshape(blocks, HB, width), left_bits, right_bits, groups, cosine)
+    scaled, errors = put(scaled, errors)
     return (
         scaled.reshape(1, local_rows, width),
         errors.reshape(1, local_rows, width // OCT),

time: 354 us -> 349 us (0.986)
  local copies, waits for them, and re-layouts: 9.4 us -> 0.52 us
    unnamed x7 -> x3, local copies, waits for them, and re-layouts: 9.4 us -> 0.52 us
    pallas_call x1 -> x2, Pallas kernels: 340 us -> 343 us  [the longest x1 340 us: body(): pl.pallas_call(functools.partial(kernel, peers, experts), out_shape=(pltp...]
where the time goes in v3:
time: 349 us
  Pallas kernels  343 us (98%)
  between operations  4.15 us (1%)
    pallas_call x1, Pallas kernels, body(): pl.pallas_call(functools.partial(kernel, peers, experts), out_shape=(pltp...  340 us

profile of v3, /device:TPU:0, one launch (start us, length us, event | category | flops | bytes accessed | tf_op | source)
XLA Modules:
  0.0 348.9 jit_solution(5953702560175287773)
XLA Ops:
  0.7 0.7 select_convert_fusion.cosine_ref
  1.4 339.8 %shard_map.83 = (bf16[14,8,16,2048]{3,2,1,0:T(8,128)(2,1)S(1)}, f32[14,8,16,256]{3,2,1,0:T(8,128)S(1)}, f32[1,16]{1,0:T(1,128)}, f32[1]{0:T(128)}, f32[1]{0:T(128)}) custom-call(bf16[14,128,2048]{2,1,0:T(8,128)(2,1)} %bitcast.4, s32[1,1792]{1,0:T(1,128)} %left_ref.1, s32[1,2048]{1,0:T(1,128)} %right_ref.1, s32[1,2048]{1,0:T(1,128)} %group_ref.1, ...), custom_call_target="tpu_custom_call" | custom-call | tf_op jit(solution)/shard_map/pallas_call | solution.py:376
  341.2 0.0 copy-start
  341.2 3.7 %shard_map.84 = (bf16[14,8,16,2048]{3,2,1,0:T(8,128)(2,1)}, f32[14,8,16,256]{3,2,1,0:T(8,128)}) custom-call(bf16[14,8,16,2048]{3,2,1,0:T(8,128)(2,1)S(1)} %get-tuple-element.12.scaled_ref, f32[14,8,16,256]{3,2,1,0:T(8,128)S(1)} %get-tuple-element.13.error_ref), custom_call_target="tpu_custom_call" | custom-call | tf_op jit(solution)/shard_map/pallas_call | solution.py:350
  344.9 0.0 copy-done
  344.9 0.5 copy.12
  (2 shorter events, 0.0 us)
Async XLA Ops:
  341.2 3.7 %copy-start = (f32[1,16]{1,0:T(1,128)S(1)}, f32[1,16]{1,0:T(1,128)}, u32[]{:S(2)}) copy-start(f32[1,16]{1,0:T(1,128)} %get-tuple-element.26) | copy-start | bytes 196
